TPU v7x, 32 devices: a 4x4x1 block of a 4x4x8 slice. The times are simulated.
32 devices in a mesh: data: 1 (over z), seq: 32 (over y, x, core).
Axes of the slice: x: 4, y: 4, z: 1, core: 2. Of those that a mesh axis runs over, the one named last changes fastest.
The devices are a block of a 4x4x8 slice.
Arguments:
- x: bfloat16 [64, 1024, 1024], P('data', 'seq')
- w_tok1: bfloat16 [2, 1024, 512], replicated
- b_tok1: float32 [2, 512], replicated
- w_tok2: bfloat16 [2, 512, 1024], replicated
- b_tok2: float32 [2, 1024], replicated
- w_ch1: bfloat16 [2, 1024, 4096], replicated
- b_ch1: float32 [2, 4096], replicated
- w_ch2: bfloat16 [2, 4096, 1024], replicated
- b_ch2: float32 [2, 1024], replicated
- ln_params: float32 [2, 4, 1024], replicated
Outputs:
- output: bfloat16 [64, 1024, 1024], P('data', 'seq')
All inputs are finite; a program needn't handle non-finite values.
Results may differ from a plain program's by a relative error of at most 0.0156138.
Values are sent between devices in bfloat16 or wider.
A program may use at most 768 MiB of HBM per device.

v0:
```python
import jax
import jax.numpy as jnp
from jax import lax
from jax.sharding import PartitionSpec as P

LN_EPS = 1e-6


def layer_norm(rows_in, ln_scale, ln_offset):
    row_vals = rows_in.astype(jnp.float32)
    row_mean = jnp.mean(row_vals, axis=-1, keepdims=True)
    centered = row_vals - row_mean
    row_var = jnp.mean(centered * centered, axis=-1, keepdims=True)
    return (centered * lax.rsqrt(row_var + LN_EPS) * ln_scale + ln_offset).astype(jnp.bfloat16)


def channel_block(act_in, t_tok, w_in, b_in, w_out, b_out, ln_layer):
    x_mid = (act_in.astype(jnp.float32) + t_tok.astype(jnp.float32)).astype(jnp.bfloat16)
    v_norm = layer_norm(x_mid, ln_layer[2], ln_layer[3])
    pre_act = jnp.einsum("bsc,ce->bse", v_norm, w_in, preferred_element_type=jnp.float32) + b_in
    a_act = jax.nn.gelu(pre_act, approximate=True).astype(jnp.bfloat16)
    ch_out = jnp.einsum("bse,ec->bsc", a_act, w_out, preferred_element_type=jnp.float32) + b_out
    return (x_mid.astype(jnp.float32) + ch_out).astype(jnp.bfloat16)


def solution(mesh):
    def local_layers(x_blk, w_tok1, b_tok1, w_tok2, b_tok2, w_ch1, b_ch1, w_ch2, b_ch2, ln_params):
        act_cur = x_blk
        for layer_idx in range(w_tok1.shape[0]):
            ln_layer = ln_params[layer_idx]
            u_norm = layer_norm(act_cur, ln_layer[0], ln_layer[1])
            u_cols = lax.all_to_all(u_norm, "seq", split_axis=2, concat_axis=1, tiled=True)
            hidden = jnp.einsum("sd,bsc->bdc", w_tok1[layer_idx], u_cols, preferred_element_type=jnp.float32)
            g_act = jax.nn.gelu(hidden + b_tok1[layer_idx][None, :, None], approximate=True).astype(jnp.bfloat16)
            t_sum = jnp.einsum("ds,bdc->bsc", w_tok2[layer_idx], g_act, preferred_element_type=jnp.float32)
            t_cols = (t_sum + b_tok2[layer_idx][None, :, None]).astype(jnp.bfloat16)
            t_rows = lax.all_to_all(t_cols, "seq", split_axis=1, concat_axis=2, tiled=True)
            act_cur = channel_block(act_cur, t_rows, w_ch1[layer_idx], b_ch1[layer_idx], w_ch2[layer_idx], b_ch2[layer_idx], ln_layer)
        return act_cur

    act_spec = P("data", "seq", None)
    rep_spec = P()
    return jax.shard_map(local_layers, mesh=mesh, in_specs=(act_spec,) + (rep_spec,) * 9, out_specs=act_spec, check_vma=False)
```

profile of v0, /device:TPU:97, one launch (start us, length us, event | category | flops | bytes accessed | tf_op | source)
XLA Modules:
  0.0 686.4 jit_solution(2536200908384973088)
XLA Ops:
  9.6 15.5 %copy.43 = bf16[64,32,1024]{0,1,2:T(8,128)(2,1)} copy(bf16[64,32,1024]{2,1,0:T(8,128)(2,1)} %fusion.47) | data formatting | bytes 8388608 | tf_op jit(solution)/shard_map/convert_element_type | solution.py:14
  25.2 13.9 %reshape.92 = bf16[32,2,32768]{2,1,0:T(2,128)(2,1)} reshape(bf16[1024,32,64]{2,1,0:T(8,128)(2,1)} %bitcast.122) | data formatting | bytes 8388608
  50.0 49.6 %all-to-all-done = bf16[32,2,32768]{2,1,0:T(2,128)(2,1)} async-done(((bf16[32,2,32768]{2,1,0:T(2,128)(2,1)}), bf16[32,2,32768]{2,1,0:T(2,128)(2,1)}, u32[]{:S(2)}, u32[]{:S(2)}) %all-to-all-start) | async-done | bytes 4194336 | tf_op jit(solution)/shard_map/all_to_all | solution.py:32
  99.6 13.7 %reshape.93 = bf16[1024,32,64]{2,1,0:T(8,128)(2,1)} reshape(bf16[32,2,32768]{2,1,0:T(2,128)(2,1)} %all-to-all-done) | data formatting | bytes 8388608
  113.3 10.5 %copy.45 = bf16[64,32,32,32]{0,3,2,1:T(8,128)(2,1)} copy(bf16[64,32,32,32]{0,2,3,1:T(8,128)(2,1)} %bitcast.126) | data formatting | bytes 8388608 | tf_op jit(solution)/shard_map/all_to_all | solution.py:32
  123.8 12.1 %copy.46 = bf16[64,1024,32]{1,2,0:T(8,128)(2,1)} copy(bf16[64,1024,32]{0,2,1:T(8,128)(2,1)} %bitcast.127) | data formatting | bytes 8388608 | tf_op jit(solution)/shard_map/all_to_all | solution.py:32
  135.9 9.8 %fusion.80 = bf16[64,1024,32]{1,2,0:T(8,128)(2,1)} fusion(f32[1024]{0:T(1024)S(1)} %bitcast.143, f32[512]{0:T(512)S(1)} %bitcast.145, bf16[64,1024,32]{1,2,0:T(8,128)(2,1)} %copy.46, bf16[2,512,1024]{2,1,0:T(8,128)(2,1)S(1)} %copy-done.13, bf16[2,1024,512]{2,1,0:T(8,128)(2,1)} %param.11), kind=kOutput, calls=%fused_computation.92 | convolution fusion | flops 4309647360 | bytes 10491904 | tf_op jit(solution)/shard_map/ds,bdc->bsc/dot_general | solution.py:35
  145.7 15.5 %copy.47 = bf16[64,1024,32]{0,2,1:T(8,128)(2,1)} copy(bf16[64,1024,32]{1,2,0:T(8,128)(2,1)} %fusion.80) | data formatting | bytes 8388608 | tf_op jit(solution)/shard_map/convert_element_type | solution.py:36
  161.3 14.3 %reshape.94 = bf16[32,2,32768]{2,1,0:T(2,128)(2,1)} reshape(bf16[1024,32,64]{2,1,0:T(8,128)(2,1)} %bitcast.123) | data formatting | bytes 8388608
  185.8 51.9 %all-to-all-done.1 = bf16[32,2,32768]{2,1,0:T(2,128)(2,1)} async-done(((bf16[32,2,32768]{2,1,0:T(2,128)(2,1)}), bf16[32,2,32768]{2,1,0:T(2,128)(2,1)}, u32[]{:S(2)}, u32[]{:S(2)}) %all-to-all-start.1) | async-done | bytes 4194336 | tf_op jit(solution)/shard_map/all_to_all | solution.py:37
  237.7 13.7 %reshape.95 = bf16[1024,32,64]{2,1,0:T(8,128)(2,1)} reshape(bf16[32,2,32768]{2,1,0:T(2,128)(2,1)} %all-to-all-done.1) | data formatting | bytes 8388608
  251.4 11.4 %convert_bitcast_fusion.1 = f32[64,32,32,32]{0,3,1,2:T(8,128)} fusion(bf16[64,32,32,32]{0,3,2,1:T(8,128)(2,1)} %bitcast.120), kind=kLoop, calls=%fused_computation.19 | loop fusion | flops 2097152 | bytes 12582912 | tf_op jit(solution)/shard_map/convert_element_type | solution.py:18
  262.8 11.9 %copy.48 = f32[64,32,32,32]{0,3,2,1:T(8,128)} copy(f32[64,32,32,32]{0,3,1,2:T(8,128)} %convert_bitcast_fusion.1) | data formatting | bytes 16777216 | tf_op jit(solution)/shard_map/convert_element_type | solution.py:18
  274.7 13.6 %copy.49 = f32[64,32,1024]{2,1,0:T(8,128)} copy(f32[64,32,1024]{0,2,1:T(8,128)} %bitcast.118) | data formatting | bytes 16777216 | tf_op jit(solution)/shard_map/convert_element_type | solution.py:18
  295.4 29.1 %fusion.109.clone.5 = bf16[64,32,4096]{2,1,0:T(8,128)(2,1)} fusion(f32[4096]{0:T(1024)S(1)} %bitcast.135, bf16[2,1024,4096]{2,1,0:T(8,128)(2,1)} %param.15, bf16[64,32,1024]{2,1,0:T(8,128)(2,1)S(1)} %get-tuple-element.8, f32[1024]{0:T(1024)S(1)} %bitcast.138, f32[1024]{0:T(1024)S(1)} %bitcast.139, ...), kind=kOutput, calls=%fused_computation.9.clone.clone.clone.clone.clone.clone.2 | convolution fusion | flops 17276338176 | bytes 29401088 | tf_op jit(solution)/shard_map/bsc,ce->bse/dot_general | solution.py:20
  324.5 23.1 %convert_reduce_fusion.1 = (f32[64,32]{1,0:T(8,128)S(1)}, bf16[64,32,1024]{2,1,0:T(8,128)(2,1)S(1)}) fusion(f32[1024]{0:T(1024)S(1)} %bitcast.142, bf16[2,4096,1024]{2,1,0:T(8,128)(2,1)} %param.17, bf16[64,32,1024]{2,1,0:T(8,128)(2,1)S(1)} %get-tuple-element.8, bf16[64,32,4096]{2,1,0:T(8,128)(2,1)} %fusion.109.clone.5), kind=kOutput, calls=%fused_computation.29 | convolution fusion | flops 17192450048 | bytes 33566720 | tf_op jit(solution)/shard_map/bse,ec->bsc/dot_general | solution.py:22
  352.7 15.5 %copy.50 = bf16[64,32,1024]{0,1,2:T(8,128)(2,1)} copy(bf16[64,32,1024]{2,1,0:T(8,128)(2,1)} %fusion.39) | data formatting | bytes 8388608 | tf_op jit(solution)/shard_map/convert_element_type | solution.py:14
  368.2 13.9 %reshape.96 = bf16[32,2,32768]{2,1,0:T(2,128)(2,1)} reshape(bf16[1024,32,64]{2,1,0:T(8,128)(2,1)} %bitcast.124) | data formatting | bytes 8388608
  382.1 61.9 %all_to_all.54 = bf16[32,2,32768]{2,1,0:T(2,128)(2,1)} all-to-all(bf16[32,2,32768]{2,1,0:T(2,128)(2,1)} %reshape.96), channel_id=1, replica_groups=mesh['data'=1,'seq'=32] {'seq'}, dimensions={0} | all-to-all | bytes 8388608 | tf_op jit(solution)/shard_map/all_to_all | solution.py:32
  443.9 13.7 %reshape.97 = bf16[1024,32,64]{2,1,0:T(8,128)(2,1)} reshape(bf16[32,2,32768]{2,1,0:T(2,128)(2,1)} %all_to_all.54) | data formatting | bytes 8388608
  457.6 10.5 %copy.52 = bf16[64,32,32,32]{0,3,2,1:T(8,128)(2,1)} copy(bf16[64,32,32,32]{0,2,3,1:T(8,128)(2,1)} %bitcast.128) | data formatting | bytes 8388608 | tf_op jit(solution)/shard_map/all_to_all | solution.py:32
  468.1 12.0 %copy.53 = bf16[64,1024,32]{1,2,0:T(8,128)(2,1)} copy(bf16[64,1024,32]{0,2,1:T(8,128)(2,1)} %bitcast.129) | data formatting | bytes 8388608 | tf_op jit(solution)/shard_map/all_to_all | solution.py:32
  480.1 9.8 %fusion.81 = bf16[64,1024,32]{1,2,0:T(8,128)(2,1)} fusion(f32[1024]{0:T(1024)S(1)} %bitcast.141, f32[512]{0:T(512)S(1)} %bitcast.144, bf16[64,1024,32]{1,2,0:T(8,128)(2,1)} %copy.53, bf16[2,512,1024]{2,1,0:T(8,128)(2,1)S(1)} %copy-done.13, bf16[2,1024,512]{2,1,0:T(8,128)(2,1)} %param.11), kind=kOutput, calls=%fused_computation.93 | convolution fusion | flops 4309647360 | bytes 10491904 | tf_op jit(solution)/shard_map/ds,bdc->bsc/dot_general | solution.py:35
  489.9 15.5 %copy.54 = bf16[64,1024,32]{0,2,1:T(8,128)(2,1)} copy(bf16[64,1024,32]{1,2,0:T(8,128)(2,1)} %fusion.81) | data formatting | bytes 8388608 | tf_op jit(solution)/shard_map/convert_element_type | solution.py:36
  505.4 14.1 %reshape.98 = bf16[32,2,32768]{2,1,0:T(2,128)(2,1)} reshape(bf16[1024,32,64]{2,1,0:T(8,128)(2,1)} %bitcast.125) | data formatting | bytes 8388608
  519.5 55.9 %all_to_all.55 = bf16[32,2,32768]{2,1,0:T(2,128)(2,1)} all-to-all(bf16[32,2,32768]{2,1,0:T(2,128)(2,1)} %reshape.98), channel_id=1, replica_groups=mesh['data'=1,'seq'=32] {'seq'}, dimensions={0} | all-to-all | bytes 8388608 | tf_op jit(solution)/shard_map/all_to_all | solution.py:37
  575.4 13.7 %reshape.99 = bf16[1024,32,64]{2,1,0:T(8,128)(2,1)} reshape(bf16[32,2,32768]{2,1,0:T(2,128)(2,1)} %all_to_all.55) | data formatting | bytes 8388608
  589.1 11.4 %convert_bitcast_fusion = f32[64,32,32,32]{0,3,1,2:T(8,128)} fusion(bf16[64,32,32,32]{0,3,2,1:T(8,128)(2,1)} %bitcast.121), kind=kLoop, calls=%fused_computation.18 | loop fusion | flops 2097152 | bytes 12582912 | tf_op jit(solution)/shard_map/convert_element_type | solution.py:18
  600.5 11.9 %copy.55 = f32[64,32,32,32]{0,3,2,1:T(8,128)} copy(f32[64,32,32,32]{0,3,1,2:T(8,128)} %convert_bitcast_fusion) | data formatting | bytes 16777216 | tf_op jit(solution)/shard_map/convert_element_type | solution.py:18
  612.4 13.6 %copy.56 = f32[64,32,1024]{2,1,0:T(8,128)} copy(f32[64,32,1024]{0,2,1:T(8,128)} %bitcast.119) | data formatting | bytes 16777216 | tf_op jit(solution)/shard_map/convert_element_type | solution.py:18
  633.1 29.1 %fusion.198 = bf16[64,32,4096]{2,1,0:T(8,128)(2,1)} fusion(f32[4096]{0:T(1024)S(1)} %bitcast.134, bf16[2,1024,4096]{2,1,0:T(8,128)(2,1)} %param.15, bf16[64,32,1024]{2,1,0:T(8,128)(2,1)S(1)} %get-tuple-element.6, f32[1024]{0:T(1024)S(1)} %bitcast.137, f32[1024]{0:T(1024)S(1)} %bitcast.136, f32[64,32]{1,0:T(8,128)S(1)} %add_rsqrt_fusion, ...), kind=kOutput, calls=%fused_computation.17.clone.clone.clone.clone.2 | convolution fusion | flops 17276338176 | bytes 29401088 | tf_op jit(solution)/shard_map/bsc,ce->bse/dot_general | solution.py:20
  662.2 23.9 %fusion.51 = bf16[64,32,1024]{2,1,0:T(8,128)(2,1)} fusion(bf16[64,32,1024]{2,1,0:T(8,128)(2,1)S(1)} %get-tuple-element.6, f32[1024]{0:T(1024)S(1)} %bitcast.140, bf16[2,4096,1024]{2,1,0:T(8,128)(2,1)} %param.17, bf16[64,32,4096]{2,1,0:T(8,128)(2,1)} %fusion.198), kind=kOutput, calls=%fused_computation.63 | convolution fusion | flops 17188257792 | bytes 33558528 | tf_op jit(solution)/shard_map/bse,ec->bsc/dot_general | solution.py:22
  (52 shorter events, 50.0 us)
Async XLA Ops:
  0.0 6.6 copy-start
  0.0 6.0 copy-start.2
  25.2 23.6 %copy-start.9 = (f32[2,512]{1,0:T(2,128)S(1)}, f32[2,512]{1,0:T(2,128)}, u32[]{:S(2)}) copy-start(f32[2,512]{1,0:T(2,128)} %param.12) | copy-start | bytes 12292
  25.2 24.3 %copy-start.5 = (f32[2,1024]{1,0:T(2,128)S(1)}, f32[2,1024]{1,0:T(2,128)}, u32[]{:S(2)}) copy-start(f32[2,1024]{1,0:T(2,128)} %param.14) | copy-start | bytes 24580
  39.1 60.6 %all-to-all-start = ((bf16[32,2,32768]{2,1,0:T(2,128)(2,1)}), bf16[32,2,32768]{2,1,0:T(2,128)(2,1)}, u32[]{:S(2)}, u32[]{:S(2)}) async-start(bf16[32,2,32768]{2,1,0:T(2,128)(2,1)} %reshape.92), calls=%async_computation | async-start | bytes 8388608 | tf_op jit(solution)/shard_map/all_to_all | solution.py:32
  123.8 12.1 %copy-start.13 = (bf16[2,512,1024]{2,1,0:T(8,128)(2,1)S(1)}, bf16[2,512,1024]{2,1,0:T(8,128)(2,1)}, u32[]{:S(2)}) copy-start(bf16[2,512,1024]{2,1,0:T(8,128)(2,1)} %param.13) | copy-start | bytes 6291460
  161.3 23.3 %copy-start.6 = (f32[2,1024]{1,0:T(2,128)S(1)}, f32[2,1024]{1,0:T(2,128)}, u32[]{:S(2)}) copy-start(f32[2,1024]{1,0:T(2,128)} %param.18) | copy-start | bytes 24580
  161.3 23.9 %copy-start.3 = (f32[2,4096]{1,0:T(2,128)S(1)}, f32[2,4096]{1,0:T(2,128)}, u32[]{:S(2)}) copy-start(f32[2,4096]{1,0:T(2,128)} %param.16) | copy-start | bytes 98308
  175.5 62.2 %all-to-all-start.1 = ((bf16[32,2,32768]{2,1,0:T(2,128)(2,1)}), bf16[32,2,32768]{2,1,0:T(2,128)(2,1)}, u32[]{:S(2)}, u32[]{:S(2)}) async-start(bf16[32,2,32768]{2,1,0:T(2,128)(2,1)} %reshape.94), calls=%async_computation.1 | async-start | bytes 8388608 | tf_op jit(solution)/shard_map/all_to_all | solution.py:37
  347.6 2.0 copy-start.1
  468.1 12.0 %copy-start.11 = (f32[1,1024]{1,0:T(1,128)S(1)}, f32[1,1024]{1,0:T(1,128)}, u32[]{:S(2)}) copy-start(f32[1,1024]{1,0:T(1,128)} %get-tuple-element.22) | copy-start | bytes 12292
  468.1 12.0 %copy-start.12 = (f32[1,512]{1,0:T(1,128)S(1)}, f32[1,512]{1,0:T(1,128)}, u32[]{:S(2)}) copy-start(f32[1,512]{1,0:T(1,128)} %get-tuple-element.24) | copy-start | bytes 6148
  626.0 7.1 %copy-start.4 = (f32[1,4096]{1,0:T(1,128)S(1)}, f32[1,4096]{1,0:T(1,128)}, u32[]{:S(2)}) copy-start(f32[1,4096]{1,0:T(1,128)} %get-tuple-element.17) | copy-start | bytes 49156
  626.0 7.1 %copy-start.7 = (f32[1,1,1024]{2,1,0:T(1,128)S(1)}, f32[1,1,1024]{2,1,0:T(1,128)}, u32[]{:S(2)}) copy-start(f32[1,1,1024]{2,1,0:T(1,128)} %get-tuple-element.9) | copy-start | bytes 12292
  626.0 7.1 %copy-start.8 = (f32[1,1,1024]{2,1,0:T(1,128)S(1)}, f32[1,1,1024]{2,1,0:T(1,128)}, u32[]{:S(2)}) copy-start(f32[1,1,1024]{2,1,0:T(1,128)} %get-tuple-element.16) | copy-start | bytes 12292
  633.1 29.1 %copy-start.10 = (f32[1,1024]{1,0:T(1,128)S(1)}, f32[1,1024]{1,0:T(1,128)}, u32[]{:S(2)}) copy-start(f32[1,1024]{1,0:T(1,128)} %get-tuple-element.19) | copy-start | bytes 12292
where the time goes:
time: 696 us; the launch traced here: 686 us
  local copies, waits for them, and re-layouts  273 us (39%)
  matrix products  125 us (18%)
  blocking collectives  118 us (17%)
  waiting for transfers between devices  101 us (15%)
  other arithmetic  50.3 us (7%)
  starting transfers between devices  18.8 us (3%)
    unnamed x36, local copies, waits for them, and re-layouts  111 us
    all_to_all x1, blocking collectives, local_layers(): lax.all_to_all(u_norm, 'seq', split_axis=2, concat_axis=1, tiled=True)  61.9 us
    dot_general x2, matrix products, channel_block(): jnp.einsum('bsc,ce->bse', v_norm, w_in, preferred_element_type=jnp.float32)  58.2 us
    all_to_all x1, blocking collectives, local_layers(): lax.all_to_all(t_cols, 'seq', split_axis=1, concat_axis=2, tiled=True)  55.9 us
    all_to_all x1, waiting for transfers between devices, local_layers(): lax.all_to_all(t_cols, 'seq', split_axis=1, concat_axis=2, tiled=True)  51.9 us
    convert_element_type x4, local copies, waits for them, and re-layouts, channel_block(): t_tok.astype(jnp.float32)  51 us
    all_to_all x1, waiting for transfers between devices, local_layers(): lax.all_to_all(u_norm, 'seq', split_axis=2, concat_axis=1, tiled=True)  49.6 us
    dot_general x2, matrix products, channel_block(): jnp.einsum('bse,ec->bsc', a_act, w_out, preferred_element_type=jnp.float32)  47.1 us
  transfers between devices with their start and end apart: 2, of which 2 were waited for; matrix products, arithmetic and copies ran while one was open for 0% of the time, Pallas kernels for 0%

commit v1 on v0

v1 whole, which is shorter than its diff:
```python
import jax
import jax.numpy as jnp
from jax import lax
from jax.sharding import PartitionSpec as P

LN_EPS = 1e-6


def layer_norm(rows_in, ln_scale, ln_offset):
    row_vals = rows_in.astype(jnp.float32)
    row_mean = jnp.mean(row_vals, axis=-1, keepdims=True)
    centered = row_vals - row_mean
    row_var = jnp.mean(centered * centered, axis=-1, keepdims=True)
    return (centered * lax.rsqrt(row_var + LN_EPS) * ln_scale + ln_offset).astype(jnp.bfloat16)


def mixer_layer(act_in, w_tok1, b_tok1, w_tok2, b_tok2, w_ch1, b_ch1, w_ch2, b_ch2, ln_layer):
    u_norm = layer_norm(act_in, ln_layer[0], ln_layer[1])
    t_imgs = []
    for img in range(act_in.shape[0]):
        hidden = jnp.einsum("sd,sc->dc", w_tok1, u_norm[img], preferred_element_type=jnp.float32)
        g_act = jax.nn.gelu(hidden + b_tok1[:, None], approximate=True).astype(jnp.bfloat16)
        t_sum = jnp.einsum("ds,dc->sc", w_tok2, g_act, preferred_element_type=jnp.float32)
        t_imgs.append((t_sum + b_tok2[:, None]).astype(jnp.bfloat16))
    t_tok = jnp.stack(t_imgs)
    x_mid = (act_in.astype(jnp.float32) + t_tok.astype(jnp.float32)).astype(jnp.bfloat16)
    v_norm = layer_norm(x_mid, ln_layer[2], ln_layer[3])
    pre_act = jnp.einsum("bsc,ce->bse", v_norm, w_ch1, preferred_element_type=jnp.float32) + b_ch1
    a_act = jax.nn.gelu(pre_act, approximate=True).astype(jnp.bfloat16)
    ch_out = jnp.einsum("bse,ec->bsc", a_act, w_ch2, preferred_element_type=jnp.float32) + b_ch2
    return (x_mid.astype(jnp.float32) + ch_out).astype(jnp.bfloat16)


def solution(mesh):
    n = mesh.shape["seq"]

    def local_layers(x_blk, w_tok1, b_tok1, w_tok2, b_tok2, w_ch1, b_ch1, w_ch2, b_ch2, ln_params):
        images, rows, chans = x_blk.shape
        mine = images // n
        got = lax.all_to_all(x_blk, "seq", split_axis=0, concat_axis=0, tiled=True)
        act = got.reshape(n, mine, rows, chans).transpose(1, 0, 2, 3).reshape(mine, n * rows, chans)
        for k in range(w_tok1.shape[0]):
            act = mixer_layer(act, w_tok1[k], b_tok1[k], w_tok2[k], b_tok2[k], w_ch1[k], b_ch1[k], w_ch2[k], b_ch2[k], ln_params[k])
        back = act.reshape(mine, n, rows, chans).transpose(1, 0, 2, 3).reshape(n * mine, rows, chans)
        return lax.all_to_all(back, "seq", split_axis=0, concat_axis=0, tiled=True)

    act_spec = P("data", "seq", None)
    rep_spec = P()
    return jax.shard_map(local_layers, mesh=mesh, in_specs=(act_spec,) + (rep_spec,) * 9, out_specs=act_spec, check_vma=False)
```

time: 696 us -> 307 us (0.44)
  local copies, waits for them, and re-layouts: 273 us -> 10.9 us
  blocking collectives: 118 us -> 60.6 us
  waiting for transfers between devices: 101 us -> 51.4 us
  other arithmetic: 50.3 us -> 26.5 us
  matrix products: 125 us -> 143 us
  starting transfers between devices: 18.8 us -> 9.22 us
    convert_element_type x8 -> x1, local copies, waits for them, and re-layouts: 113 us -> 3.23 us  [mixer_layer(): act_in.astype(jnp.float32) + t_tok.astype(jnp.float32)]
    unnamed x36 -> x25, local copies, waits for them, and re-layouts: 111 us -> 6.35 us
    all_to_all x2 -> x1, blocking collectives: 118 us -> 60.6 us  [local_layers(): return lax.all_to_all(back, 'seq', split_axis=0, concat_axis=0, tiled=True)]
    all_to_all x2 -> x1, waiting for transfers between devices: 101 us -> 51.4 us  [local_layers(): got = lax.all_to_all(x_blk, 'seq', split_axis=0, concat_axis=0, tiled=True)]
    all_to_all x4 -> x0, local copies, waits for them, and re-layouts: 45.1 us -> none  [local_layers(): lax.all_to_all(u_norm, 'seq', split_axis=2, concat_axis=1, tiled=True)]
    convert_element_type x2 -> x1, other arithmetic: 22.8 us -> 3.21 us  [mixer_layer(): act_in.astype(jnp.float32) + t_tok.astype(jnp.float32)]
    dot_general x6 -> x8, matrix products: 125 us -> 143 us  [the longest x2 72.6 us: mixer_layer(): jnp.einsum('bsc,ce->bse', v_norm, w_ch1, preferred_element_type=jnp.float32)]
    all_to_all x2 -> x1, starting transfers between devices: 18.8 us -> 9.22 us  [local_layers(): got = lax.all_to_all(x_blk, 'seq', split_axis=0, concat_axis=0, tiled=True)]
  transfers between devices with their start and end apart: 2 -> 1, of which waited for: 2 -> 1; matrix products, arithmetic and copies ran while one was open for 0% -> 0% of each run, Pallas kernels for 0% -> 0%
where the time goes in v1:
time: 307 us; the launch traced here: 302 us
  matrix products  143 us (47%)
  blocking collectives  60.6 us (20%)
  waiting for transfers between devices  51.4 us (17%)
  other arithmetic  26.5 us (9%)
  local copies, waits for them, and re-layouts  10.9 us (4%)
  starting transfers between devices  9.22 us (3%)
    dot_general x2, matrix products, mixer_layer(): jnp.einsum('bsc,ce->bse', v_norm, w_ch1, preferred_element_type=jnp.float32)  72.6 us
    all_to_all x1, blocking collectives, local_layers(): return lax.all_to_all(back, 'seq', split_axis=0, concat_axis=0, tiled=True)  60.6 us
    all_to_all x1, waiting for transfers between devices, local_layers(): got = lax.all_to_all(x_blk, 'seq', split_axis=0, concat_axis=0, tiled=True)  51.4 us
    dot_general x2, matrix products, mixer_layer(): jnp.einsum('bse,ec->bsc', a_act, w_ch2, preferred_element_type=jnp.float32)  47 us
    dot_general x4, matrix products, mixer_layer(): jnp.einsum('ds,dc->sc', w_tok2, g_act, preferred_element_type=jnp.float32)  23.1 us
    all_to_all x1, starting transfers between devices, local_layers(): got = lax.all_to_all(x_blk, 'seq', split_axis=0, concat_axis=0, tiled=True)  9.22 us
    convert_element_type x3, other arithmetic, layer_norm(): (centered * lax.rsqrt(row_var + LN_EPS) * ln_scale + ln_offset).astype(jn...  8.73 us
    reduce_sum x3, other arithmetic, layer_norm(): row_mean = jnp.mean(row_vals, axis=-1, keepdims=True)  8.69 us
  transfers between devices with their start and end apart: 1, of which 1 were waited for; matrix products, arithmetic and copies ran while one was open for 0% of the time, Pallas kernels for 0%

profile of v1, /device:TPU:97, one launch (start us, length us, event | category | flops | bytes accessed | tf_op | source)
XLA Modules:
  0.0 302.0 jit_solution(3216163284346623066)
XLA Ops:
  0.0 9.2 %all-to-all-start = ((bf16[64,32,1024]{2,1,0:T(8,128)(2,1)}), bf16[64,32,1024]{2,1,0:T(8,128)(2,1)}, u32[]{:S(2)}, u32[]{:S(2)}) async-start(bf16[64,32,1024]{2,1,0:T(8,128)(2,1)} %param.10), calls=%async_computation | async-start | bytes 8388608 | tf_op jit(solution)/shard_map/all_to_all | solution.py:40
  9.3 0.6 fusion.183
  10.0 51.4 %all-to-all-done = bf16[64,32,1024]{2,1,0:T(8,128)(2,1)} async-done(((bf16[64,32,1024]{2,1,0:T(8,128)(2,1)}), bf16[64,32,1024]{2,1,0:T(8,128)(2,1)}, u32[]{:S(2)}, u32[]{:S(2)}) %all-to-all-start) | async-done | bytes 4194336 | tf_op jit(solution)/shard_map/all_to_all | solution.py:40
  61.3 3.2 %bitcast_convert_fusion = f32[32,2,32,1024]{3,2,1,0:T(8,128)S(1)} fusion(bf16[64,32,1024]{2,1,0:T(8,128)(2,1)} %all-to-all-done), kind=kLoop, calls=%fused_computation.179 | loop fusion | flops 2097152 | bytes 12582912 | tf_op jit(solution)/shard_map/convert_element_type | solution.py:26
  64.6 0.4 bitcast_reduce_fusion
  65.0 2.8 copy-done
  67.8 1.1 fusion.57
  68.9 0.1 div.27
  69.0 0.1 rsqrt.36
  69.1 3.2 %copy.11 = f32[32,2,32,1024]{3,2,0,1:T(8,128)S(1)} copy(bf16[32,2,32,1024]{3,2,1,0:T(8,128)(2,1)} %bitcast.54) | data formatting | bytes 12582912 | tf_op jit(solution)/shard_map/convert_element_type | solution.py:26
  72.4 4.0 %fusion.53 = bf16[2,1024,1024]{2,1,0:T(8,128)(2,1)} fusion(f32[32,2,32,1024]{3,2,0,1:T(8,128)S(1)} %copy.11, f32[1024]{0:T(1024)S(1)} %bitcast.203, f32[1024]{0:T(1024)S(1)} %bitcast.204, f32[2,1024]{1,0:T(2,128)S(1)} %rsqrt.36, f32[2,1024]{1,0:T(2,128)S(1)} %div.27), kind=kLoop, calls=%fused_computation.59 | loop fusion | flops 10485760 | bytes 12607488 | tf_op jit(solution)/shard_map/convert_element_type | solution.py:14
  76.4 0.5 copy-done.3
  76.9 4.9 %add_convert_fusion.4 = bf16[1024,1024]{0,1:T(8,128)(2,1)S(1)} fusion(f32[1024]{0:T(1024)S(1)} %bitcast.213, bf16[2,1024,1024]{2,1,0:T(8,128)(2,1)} %fusion.53, f32[512]{0:T(512)S(1)} %bitcast.217, bf16[2,512,1024]{2,1,0:T(8,128)(2,1)} %param.13, bf16[2,1024,512]{2,1,0:T(8,128)(2,1)} %param.11), kind=kOutput, calls=%fused_computation.79 | convolution fusion | flops 2154823680 | bytes 6297600 | tf_op jit(solution)/shard_map/ds,dc->sc/dot_general | solution.py:23
  81.8 7.1 %add_convert_fusion.3 = bf16[1024,1024]{0,1:T(8,128)(2,1)} fusion(f32[1024]{0:T(1024)S(1)} %bitcast.214, bf16[2,1024,1024]{2,1,0:T(8,128)(2,1)} %fusion.53, f32[512]{0:T(512)S(1)} %bitcast.218, bf16[2,512,1024]{2,1,0:T(8,128)(2,1)} %param.13, bf16[2,1024,512]{2,1,0:T(8,128)(2,1)} %param.11), kind=kOutput, calls=%fused_computation.78 | convolution fusion | flops 2154823680 | bytes 6297600 | tf_op jit(solution)/shard_map/ds,dc->sc/dot_general | solution.py:23
  88.8 4.6 %convert_reduce_fusion.2 = (f32[2,32,32]{2,1,0:T(8,128)S(1)}, bf16[2,32,32,1024]{3,2,1,0:T(8,128)(2,1)S(1)}) fusion(bf16[1,32,32,1024]{3,2,1,0:T(8,128)(2,1)} %bitcast.197, bf16[1,32,32,1024]{3,2,1,0:T(8,128)(2,1)S(1)} %bitcast.195, f32[32,2,32,1024]{3,2,1,0:T(8,128)} %copy-done), kind=kLoop, calls=%fused_computation.29 | loop fusion | flops 12580864 | bytes 16785408 | tf_op jit(solution)/shard_map/reduce_sum | solution.py:11
  93.5 1.4 fusion.38
  94.9 1.7 fusion.41
  96.7 39.7 %fusion.87.clone.5 = bf16[2,1024,4096]{2,1,0:T(8,128)(2,1)} fusion(f32[4096]{0:T(1024)S(1)} %bitcast.206, bf16[2,1024,1024]{2,1,0:T(8,128)(2,1)S(1)} %bitcast.193, bf16[2,1024,4096]{2,1,0:T(8,128)(2,1)} %param.15), kind=kOutput, calls=%fused_computation.9.clone.clone.clone.clone.clone.clone.2 | convolution fusion | flops 17263755264 | bytes 29376512 | tf_op jit(solution)/shard_map/bsc,ce->bse/dot_general | solution.py:28
  136.4 24.2 %convert_reduce_fusion.1 = (f32[2,1024]{1,0:T(2,128)S(1)}, bf16[2,1024,1024]{2,1,0:T(8,128)(2,1)S(1)}) fusion(f32[1024]{0:T(1024)S(1)} %bitcast.212, bf16[2,4096,1024]{2,1,0:T(8,128)(2,1)} %param.17, bf16[1,1024,1024]{2,1,0:T(8,128)(2,1)} %bitcast.198, bf16[1,1024,1024]{2,1,0:T(8,128)(2,1)} %bitcast.196, f32[32,2,32,1024]{3,2,0,1:T(8,128)} %copy-done.3, ...), kind=kOutput, calls=%fused_computation.27 | convolution fusion | flops 17200838656 | bytes 41955328 | tf_op jit(solution)/shard_map/bse,ec->bsc/dot_general | solution.py:30
  160.6 1.4 fusion.34
  162.0 3.0 fusion.37
  165.0 4.9 %fusion.124 = bf16[1,1024,1024]{2,1,0:T(8,128)(2,1)S(1)} fusion(f32[1024]{0:T(1024)S(1)} %bitcast.210, bf16[2,1024,1024]{2,1,0:T(8,128)(2,1)} %fusion.37, f32[512]{0:T(512)S(1)} %bitcast.215, bf16[2,512,1024]{2,1,0:T(8,128)(2,1)} %param.13, bf16[2,1024,512]{2,1,0:T(8,128)(2,1)} %param.11), kind=kOutput, calls=%fused_computation.124 | convolution fusion | flops 2154823680 | bytes 6297600 | tf_op jit(solution)/shard_map/ds,dc->sc/dot_general | solution.py:23
  169.9 6.2 %fusion.125 = bf16[1,1024,1024]{2,1,0:T(8,128)(2,1)} fusion(f32[1024]{0:T(1024)S(1)} %bitcast.211, bf16[2,1024,1024]{2,1,0:T(8,128)(2,1)} %fusion.37, f32[512]{0:T(512)S(1)} %bitcast.216, bf16[2,512,1024]{2,1,0:T(8,128)(2,1)} %param.13, bf16[2,1024,512]{2,1,0:T(8,128)(2,1)} %param.11), kind=kOutput, calls=%fused_computation.125 | convolution fusion | flops 2154823680 | bytes 6297600 | tf_op jit(solution)/shard_map/ds,dc->sc/dot_general | solution.py:23
  176.1 3.6 %convert_reduce_fusion = f32[2,1024]{1,0:T(2,128)S(1)} fusion(bf16[1,1024,1024]{2,1,0:T(8,128)(2,1)} %fusion.125, bf16[1,1024,1024]{2,1,0:T(8,128)(2,1)S(1)} %fusion.124, bf16[2,1024,1024]{2,1,0:T(8,128)(2,1)} %copy-done.1), kind=kLoop, calls=%fused_computation.24 | loop fusion | flops 14678016 | bytes 8396800 | tf_op jit(solution)/shard_map/reduce_sum | solution.py:11
  179.8 0.4 copy-done.2
  180.2 0.7 copy-done.4
  180.9 1.8 fusion.30
  182.7 32.9 %fusion.212 = bf16[2,1024,4096]{2,1,0:T(8,128)(2,1)} fusion(f32[4096]{0:T(1024)S(1)} %bitcast.205, bf16[2,1024,4096]{2,1,0:T(8,128)(2,1)} %param.15, f32[1024]{0:T(1024)S(1)} %bitcast.207, f32[1024]{0:T(1024)S(1)} %bitcast.208, f32[2,1024]{1,0:T(2,128)S(1)} %add_rsqrt_fusion.2, f32[2,1024]{1,0:T(2,128)S(1)} %broadcast_multiply_fusion.2, ...), kind=kOutput, calls=%fused_computation.17.clone.clone.clone.clone.2 | convolution fusion | flops 17286823936 | bytes 33595392 | tf_op jit(solution)/shard_map/bsc,ce->bse/dot_general | solution.py:28
  215.6 22.9 %fusion.43 = bf16[2,1024,1024]{2,1,0:T(8,128)(2,1)S(1)} fusion(f32[1024]{0:T(1024)S(1)} %bitcast.209, bf16[2,4096,1024]{2,1,0:T(8,128)(2,1)} %param.17, bf16[1,1024,1024]{2,1,0:T(8,128)(2,1)S(1)} %copy-done.4, bf16[1,1024,1024]{2,1,0:T(8,128)(2,1)S(1)} %fusion.124, bf16[2,1024,1024]{2,1,0:T(8,128)(2,1)S(1)} %copy-done.2, bf16[2,1024,4096]{2,1,0:T(8,128)(2,1)} %fusion.212), kind=kOutput, calls=%fused_computation.49 | convolution fusion | flops 17198743552 | bytes 37752832 | tf_op jit(solution)/shard_map/bse,ec->bsc/dot_general | solution.py:30
  238.5 0.5 copy.12
  239.1 60.6 %all_to_all.10 = bf16[64,32,1024]{2,1,0:T(8,128)(2,1)S(1)} all-to-all(bf16[64,32,1024]{2,1,0:T(8,128)(2,1)S(1)} %bitcast.192), channel_id=1, replica_groups=mesh['data'=1,'seq'=32] {'seq'}, dimensions={0} | all-to-all | bytes 8388608 | tf_op jit(solution)/shard_map/all_to_all | solution.py:45
  299.6 2.0 copy.18
  (32 shorter events, 0.2 us)
Async XLA Ops:
  0.0 9.3 %copy-start.10 = (f32[2,512]{1,0:T(2,128)S(1)}, f32[2,512]{1,0:T(2,128)}, u32[]{:S(2)}) copy-start(f32[2,512]{1,0:T(2,128)} %param.12) | copy-start | bytes 12292
  0.0 9.3 %copy-start.8 = (f32[2,1024]{1,0:T(2,128)S(1)}, f32[2,1024]{1,0:T(2,128)}, u32[]{:S(2)}) copy-start(f32[2,1024]{1,0:T(2,128)} %param.14) | copy-start | bytes 24580
  0.0 9.3 %copy-start.9 = (f32[2,1024]{1,0:T(2,128)S(1)}, f32[2,1024]{1,0:T(2,128)}, u32[]{:S(2)}) copy-start(f32[2,1024]{1,0:T(2,128)} %param.18) | copy-start | bytes 24580
  0.0 9.9 %copy-start.6 = (f32[2,4,1024]{2,1,0:T(4,128)S(1)}, f32[2,4,1024]{2,1,0:T(4,128)}, u32[]{:S(2)}) copy-start(f32[2,4,1024]{2,1,0:T(4,128)} %param.19) | copy-start | bytes 98308
  0.0 9.9 %copy-start.7 = (f32[2,4096]{1,0:T(2,128)S(1)}, f32[2,4096]{1,0:T(2,128)}, u32[]{:S(2)}) copy-start(f32[2,4096]{1,0:T(2,128)} %param.16) | copy-start | bytes 98308
  0.0 61.3 %all-to-all-start = ((bf16[64,32,1024]{2,1,0:T(8,128)(2,1)}), bf16[64,32,1024]{2,1,0:T(8,128)(2,1)}, u32[]{:S(2)}, u32[]{:S(2)}) async-start(bf16[64,32,1024]{2,1,0:T(8,128)(2,1)} %param.10), calls=%async_computation | async-start | bytes 8388608 | tf_op jit(solution)/shard_map/all_to_all | solution.py:40
  64.6 3.2 %copy-start = (f32[32,2,32,1024]{3,2,1,0:T(8,128)}, f32[32,2,32,1024]{3,2,1,0:T(8,128)S(1)}, u32[]{:S(2)}) copy-start(f32[32,2,32,1024]{3,2,1,0:T(8,128)S(1)} %bitcast_convert_fusion) | copy-start | bytes 25165828
  72.4 4.5 %copy-start.3 = (f32[32,2,32,1024]{3,2,0,1:T(8,128)}, f32[32,2,32,1024]{3,2,0,1:T(8,128)S(1)}, u32[]{:S(2)}) copy-start(f32[32,2,32,1024]{3,2,0,1:T(8,128)S(1)} %copy.11) | copy-start | bytes 25165828
  81.8 7.1 %copy-start.5 = (bf16[1024,1024]{0,1:T(8,128)(2,1)}, bf16[1024,1024]{0,1:T(8,128)(2,1)S(1)}, u32[]{:S(2)}) copy-start(bf16[1024,1024]{0,1:T(8,128)(2,1)S(1)} %add_convert_fusion.4) | copy-start | bytes 6291460
  160.6 4.4 %copy-start.1 = (bf16[2,1024,1024]{2,1,0:T(8,128)(2,1)}, bf16[2,1024,1024]{2,1,0:T(8,128)(2,1)S(1)}, u32[]{:S(2)}) copy-start(bf16[2,1024,1024]{2,1,0:T(8,128)(2,1)S(1)} %get-tuple-element.24) | copy-start | bytes 12582916
  176.1 4.1 %copy-start.2 = (bf16[2,1024,1024]{2,1,0:T(8,128)(2,1)S(1)}, bf16[2,1024,1024]{2,1,0:T(8,128)(2,1)}, u32[]{:S(2)}) copy-start(bf16[2,1024,1024]{2,1,0:T(8,128)(2,1)} %copy-done.1) | copy-start | bytes 12582916
  176.1 4.7 %copy-start.4 = (bf16[1,1024,1024]{2,1,0:T(8,128)(2,1)S(1)}, bf16[1,1024,1024]{2,1,0:T(8,128)(2,1)}, u32[]{:S(2)}) copy-start(bf16[1,1024,1024]{2,1,0:T(8,128)(2,1)} %fusion.125) | copy-start | bytes 6291460
  182.7 32.9 %copy-start.11 = (f32[1,1024]{1,0:T(1,128)S(1)}, f32[1,1024]{1,0:T(1,128)}, u32[]{:S(2)}) copy-start(f32[1,1024]{1,0:T(1,128)} %get-tuple-element.18) | copy-start | bytes 12292

commit v2 on v1

v2 whole, which is shorter than its diff:
```python
import functools

import jax
import jax.numpy as jnp
from jax import lax
from jax.experimental import pallas as pl
from jax.experimental.pallas import tpu as pltpu
from jax.sharding import PartitionSpec as P

LN_EPS = 1e-6
GELU_A = 0.7978845608028654
GELU_B = GELU_A * 0.044715
MESH = pl.DeviceIdType.MESH
BF16 = jnp.bfloat16
F32 = jnp.float32
LN_ROWS = 16


def gelu(h):
    half = 0.5 * h
    return half + half * jnp.tanh(h * (GELU_A + GELU_B * (h * h)))


def norm_rows(rows, gamma, beta):
    mean = jnp.mean(rows, axis=-1, keepdims=True)
    cent = rows - mean
    var = jnp.mean(cent * cent, axis=-1, keepdims=True)
    return (cent * lax.rsqrt(var + LN_EPS) * gamma + beta).astype(BF16)


def mixer_kernel(
    n, x_ref, wt1_ref, bt1_ref, wt2_ref, bt2_ref, wc1_ref, bc1_ref, wc2_ref, bc2_ref, ln_ref,
    out_ref, xb, w1t, w2t, s1, s2, wc1, wc2, ub, acc, ab, b1c, b2c,
    in_send, in_recv, out_send, out_recv, tok_sem, ch_sem,
):
    me = lax.axis_index("seq")
    images, rows, chans = x_ref.shape
    mine = images // n
    layers, patches, tok_hidden = wt1_ref.shape
    ch_hidden = wc1_ref.shape[2]
    blk = ub.shape[0] // 2
    blocks = patches // blk
    per_blk = n // blocks
    echunk = ab.shape[2]
    nchunk = ch_hidden // echunk

    barrier = pltpu.get_barrier_semaphore()

    def signal_peer(k, carry):
        pl.semaphore_signal(barrier, inc=1, device_id={"seq": lax.rem(me + k, n)}, device_id_type=MESH)
        return carry

    lax.fori_loop(1, n, signal_peer, 0)

    tok_copies = [pltpu.make_async_copy(wt1_ref, s1, tok_sem.at[0]), pltpu.make_async_copy(wt2_ref, s2, tok_sem.at[1])]
    for copy in tok_copies:
        copy.start()
    pl.semaphore_wait(barrier, n - 1)

    def send_in(img):
        def one(k, carry):
            peer = lax.rem(me + lax.rem(k * 11, n), n)
            pltpu.make_async_remote_copy(
                src_ref=x_ref.at[peer * mine + img],
                dst_ref=xb.at[img, pl.ds(me * rows, rows)],
                send_sem=in_send.at[img],
                recv_sem=in_recv.at[img],
                device_id={"seq": peer},
                device_id_type=MESH,
            ).start()
            return carry

        lax.fori_loop(1, n, one, 0)
        pltpu.make_async_copy(x_ref.at[me * mine + img], xb.at[img, pl.ds(me * rows, rows)], in_recv.at[img]).start()

    send_in(0)
    for k in range(layers):
        pltpu.make_async_copy(wc1_ref.at[k], wc1.at[k], ch_sem.at[0, k]).start()
        pltpu.make_async_copy(wc2_ref.at[k], wc2.at[k], ch_sem.at[1, k]).start()

    for copy in tok_copies:
        copy.wait()
    tile = 256

    def flip(k, carry):
        for r in range(0, patches, tile):
            w1t[k, :, r : r + tile] = s1[k, r : r + tile, :].T
        for r in range(0, tok_hidden, tile):
            w2t[k, :, r : r + tile] = s2[k, r : r + tile, :].T
        b1c[k] = jnp.broadcast_to(bt1_ref[pl.ds(k, 1), :], (128, tok_hidden)).T
        b2c[k] = jnp.broadcast_to(bt2_ref[pl.ds(k, 1), :], (128, patches)).T
        return carry

    lax.fori_loop(0, layers, flip, 0)

    def peer_of(b, g):
        core = g % 2
        pair = g // 2
        row = pair // 2
        parity = lax.rem(me // 2 + me // 8 + b + row, 2)
        return (pair * 2 + parity) * 2 + core

    def send_out(img, b):
        def one(g, carry):
            peer = peer_of(b, g)

            @pl.when(peer == me)
            def _():
                pltpu.make_async_copy(xb.at[img, pl.ds(peer * rows, rows)], out_ref.at[me * mine + img], out_recv.at[0]).start()

            @pl.when(peer != me)
            def _():
                pltpu.make_async_remote_copy(
                    src_ref=xb.at[img, pl.ds(peer * rows, rows)],
                    dst_ref=out_ref.at[me * mine + img],
                    send_sem=out_send.at[0],
                    recv_sem=out_recv.at[0],
                    device_id={"seq": peer},
                    device_id_type=MESH,
                ).start()

            return carry

        lax.fori_loop(0, per_blk, one, 0)

    def layer_step(step, carry):
        img = step // layers
        k = lax.rem(step, layers)

        @pl.when(k == 0)
        def _():
            pltpu.make_async_copy(xb.at[img], xb.at[img], in_recv.at[img]).wait()

        @pl.when((k == 0) & (img + 1 < mine))
        def _():
            send_in(img + 1)

        gamma1, beta1 = ln_ref[k, pl.ds(0, 1), :], ln_ref[k, pl.ds(1, 1), :]

        def ln1(r, c):
            at = pl.ds(pl.multiple_of(r * LN_ROWS, LN_ROWS), LN_ROWS)
            ub[at, :] = norm_rows(xb[img, at, :].astype(F32), gamma1, beta1)
            return c

        lax.fori_loop(0, patches // LN_ROWS, ln1, 0, unroll=4)

        half = chans // 2
        gs = []
        for c in range(0, chans, half):
            h = jnp.dot(w1t[k], ub[:, c : c + half], preferred_element_type=F32) + b1c[k, :, 0:1]
            gs.append(gelu(h).astype(BF16))
        for c, g in zip(range(0, chans, half), gs):
            t = (jnp.dot(w2t[k], g, preferred_element_type=F32) + b2c[k, :, 0:1]).astype(BF16)
            xb[img, :, c : c + half] = (xb[img, :, c : c + half].astype(F32) + t.astype(F32)).astype(BF16)

        @pl.when(img == 0)
        def _():
            pltpu.make_async_copy(wc1_ref.at[k], wc1.at[k], ch_sem.at[0, k]).wait()
            pltpu.make_async_copy(wc2_ref.at[k], wc2.at[k], ch_sem.at[1, k]).wait()

        gamma2, beta2, bias2 = ln_ref[k, pl.ds(2, 1), :], ln_ref[k, pl.ds(3, 1), :], bc2_ref[pl.ds(k, 1), :]

        def channel_block(b, c0):
            def ln2(g, c):
                at = pl.multiple_of(peer_of(b, g) * rows, rows)
                to = pl.multiple_of(g * rows, rows)
                for r in range(0, rows, LN_ROWS):
                    vals = xb[img, pl.ds(at + r, LN_ROWS), :].astype(F32)
                    ub[pl.ds(to + r, LN_ROWS), :] = norm_rows(vals, gamma2, beta2)
                    acc[pl.ds(to + r, LN_ROWS), :] = vals + bias2
                return c

            lax.fori_loop(0, per_blk, ln2, 0, unroll=2)

            def up(e, slot):
                cols = pl.ds(pl.multiple_of(e * echunk, echunk), echunk)
                h = jnp.dot(ub[0:blk, :], wc1[k, :, cols], preferred_element_type=F32) + bc1_ref[pl.ds(k, 1), cols]
                ab[slot] = gelu(h).astype(BF16)

            def down(e, slot):
                at = pl.ds(pl.multiple_of(e * echunk, echunk), echunk)
                return acc[...] + jnp.dot(ab[slot], wc2[k, at, :], preferred_element_type=F32)

            up(0, 0)

            def mid(e, c):
                acc[...] = down(e - 1, lax.rem(e - 1, 2))
                up(e, lax.rem(e, 2))
                return c

            lax.fori_loop(1, nchunk, mid, 0)
            z = down(nchunk - 1, (nchunk - 1) % 2).astype(BF16)
            for g in range(per_blk):
                at = pl.multiple_of(peer_of(b, g) * rows, rows)
                xb[img, pl.ds(at, rows), :] = z[g * rows : (g + 1) * rows]

            @pl.when(k == layers - 1)
            def _():
                send_out(img, b)

            return c0

        lax.fori_loop(0, blocks, channel_block, 0)
        return carry

    lax.fori_loop(0, mine * layers, layer_step, 0)

    for img in range(mine):
        pltpu.make_async_copy(x_ref.at[pl.ds(0, n - 1)], x_ref.at[pl.ds(0, n - 1)], in_send.at[img]).wait()
    sent = x_ref.at[pl.ds(0, mine * (n - 1))]
    pltpu.make_async_copy(sent, sent, out_send.at[0]).wait()
    pltpu.make_async_copy(out_ref, out_ref, out_recv.at[0]).wait()


def solution(mesh):
    n = mesh.shape["seq"]

    def local_layers(x_blk, w_tok1, b_tok1, w_tok2, b_tok2, w_ch1, b_ch1, w_ch2, b_ch2, ln_params):
        images, rows, chans = x_blk.shape
        mine = images // n
        layers, patches, tok_hidden = w_tok1.shape
        ch_hidden = w_ch1.shape[2]
        blk = patches // 2
        hbm = pl.BlockSpec(memory_space=pl.ANY)
        vmem = pl.BlockSpec(memory_space=pltpu.VMEM)
        flops = 4 * mine * layers * patches * chans * (tok_hidden + ch_hidden)
        dma = pltpu.SemaphoreType.DMA
        return pl.pallas_call(
            functools.partial(mixer_kernel, n),
            out_shape=jax.ShapeDtypeStruct(x_blk.shape, x_blk.dtype),
            in_specs=[hbm, hbm, vmem, hbm, vmem, hbm, vmem, hbm, vmem, vmem],
            out_specs=hbm,
            scratch_shapes=[
                pltpu.VMEM((mine, patches, chans), BF16),
                pltpu.VMEM((layers, tok_hidden, patches), BF16),
                pltpu.VMEM((layers, patches, tok_hidden), BF16),
                pltpu.VMEM((layers, patches, tok_hidden), BF16),
                pltpu.VMEM((layers, tok_hidden, patches), BF16),
                pltpu.VMEM((layers, chans, ch_hidden), BF16),
                pltpu.VMEM((layers, ch_hidden, chans), BF16),
                pltpu.VMEM((patches, chans), BF16),
                pltpu.VMEM((blk, chans), F32),
                pltpu.VMEM((2, blk, chans), BF16),
                pltpu.VMEM((layers, tok_hidden, 128), F32),
                pltpu.VMEM((layers, patches, 128), F32),
                dma((mine,)),
                dma((mine,)),
                dma((1,)),
                dma((1,)),
                dma((2,)),
                dma((2, layers)),
            ],
            compiler_params=pltpu.CompilerParams(collective_id=0, has_side_effects=True, vmem_limit_bytes=67043328),
            cost_estimate=pl.CostEstimate(flops=flops, bytes_accessed=2 * x_blk.size * 2, transcendentals=0),
        )(x_blk, w_tok1, b_tok1, w_tok2, b_tok2, w_ch1, b_ch1, w_ch2, b_ch2, ln_params)

    act_spec = P("data", "seq", None)
    rep_spec = P()
    return jax.shard_map(local_layers, mesh=mesh, in_specs=(act_spec,) + (rep_spec,) * 9, out_specs=act_spec, check_vma=False)
```

time: 307 us -> 189 us (0.62)
  the two profiles are of different devices: /device:TPU:97 before, /device:TPU:121 now
where the time goes in v2:
time: 189 us
  Pallas kernels  184 us (97%)
  local copies, waits for them, and re-layouts  5.01 us (3%)
    pallas_call x1, Pallas kernels, local_layers(): pl.pallas_call(functools.partial(mixer_kernel, n), out_shape=jax.ShapeDty...  184 us
    unnamed x1, local copies, waits for them, and re-layouts  5.01 us

profile of v2, /device:TPU:121, one launch (start us, length us, event | category | flops | bytes accessed | tf_op | source)
XLA Modules:
  0.0 189.1 jit_solution(1051792655515427705)
XLA Ops:
  0.0 184.1 %shard_map.100 = bf16[64,32,1024]{2,1,0:T(8,128)(2,1)} custom-call(bf16[64,32,1024]{2,1,0:T(8,128)(2,1)} %x_ref.1, bf16[2,1024,512]{2,1,0:T(8,128)(2,1)} %wt1_ref.1, f32[2,512]{1,0:T(2,128)} %bt1_ref.1, bf16[2,512,1024]{2,1,0:T(8,128)(2,1)} %wt2_ref.1, f32[2,1024]{1,0:T(2,128)} %bt2_ref.1, bf16[2,1024,4096]{2,1,0:T(8,128)(2,1)} %wc1_ref.1, ...), custom_call_target="tpu_custom_call" | custom-call | flops 77309411328 | bytes 8388608 | tf_op jit(solution)/shard_map/pallas_call | solution.py:228
  184.1 5.0 %copy.12 = bf16[64,32,1024]{2,1,0:T(8,128)(2,1)} copy(bf16[64,32,1024]{2,1,0:T(8,128)(2,1)} %shard_map.100) | data formatting | bytes 8388608

commit v3 on v2

v3 whole, which is shorter than its diff:
```python
import functools

import jax
import jax.numpy as jnp
from jax import lax
from jax.experimental import pallas as pl
from jax.experimental.pallas import tpu as pltpu
from jax.sharding import PartitionSpec as P

LN_EPS = 1e-6
GELU_A = 0.7978845608028654
GELU_B = GELU_A * 0.044715
MESH = pl.DeviceIdType.MESH
BF16 = jnp.bfloat16
F32 = jnp.float32
LN_ROWS = 16
UNROLL = 4
ECHUNK = 1024


def gelu(h):
    half = 0.5 * h
    return half + half * jnp.tanh(h * (GELU_A + GELU_B * (h * h)))


def norm_rows(rows, gamma, beta):
    mean = jnp.mean(rows, axis=-1, keepdims=True)
    cent = rows - mean
    var = jnp.mean(cent * cent, axis=-1, keepdims=True)
    return (cent * lax.rsqrt(var + LN_EPS) * gamma + beta).astype(BF16)


def mixer_kernel(
    n, x_ref, wt1_ref, bt1_ref, wt2_ref, bt2_ref, wc1_ref, bc1_ref, wc2_ref, bc2_ref, ln_ref,
    out_ref, state, w1t, w2t, s1, s2, wc1, wc2, ub, gb, acc, ab, b1c, b2c,
    in_send, in_recv, mid_send, mid_recv, out_sem, tok_sem, ch_sem,
):
    me = lax.axis_index("seq")
    images, rows, chans = x_ref.shape
    mine = images // n
    layers, patches, tok_hidden = wt1_ref.shape
    ch_hidden = wc1_ref.shape[2]
    halves = 2
    blk = patches // halves
    per_blk = n // halves
    echunk = ab[0].shape[1]
    nchunk = ch_hidden // echunk
    my_parity = me // 2 + me // 8
    my_place = (me // 4) * 2 + lax.rem(me, 2)

    def peer_at(b, place):
        pair = place // 2
        return pair * 4 + lax.rem(my_parity + b + pair // 2, 2) * 2 + lax.rem(place, 2)

    def turn(i):
        return lax.rem(my_place + i * 5, per_blk)

    barrier = pltpu.get_barrier_semaphore()

    def signal_peer(i, carry):
        pl.semaphore_signal(barrier, inc=1, device_id={"seq": lax.rem(me + i, n)}, device_id_type=MESH)
        return carry

    lax.fori_loop(1, n, signal_peer, 0)

    tok_copies = [pltpu.make_async_copy(wt1_ref, s1, tok_sem.at[0]), pltpu.make_async_copy(wt2_ref, s2, tok_sem.at[1])]
    for copy in tok_copies:
        copy.start()
    pl.semaphore_wait(barrier, n - 1)

    def send_in(img):
        for b in range(halves):
            def one(i, carry, b=b):
                peer = peer_at(b, turn(i))
                pltpu.make_async_remote_copy(
                    src_ref=x_ref.at[peer * mine + img],
                    dst_ref=state.at[img, pl.ds(me * rows, rows)],
                    send_sem=in_send.at[img],
                    recv_sem=in_recv.at[img, b],
                    device_id={"seq": peer},
                    device_id_type=MESH,
                ).start()
                return carry

            if b == 0:
                pltpu.make_async_copy(x_ref.at[me * mine + img], state.at[img, pl.ds(me * rows, rows)], in_recv.at[img, b]).start()
            lax.fori_loop(1 if b == 0 else 0, per_blk, one, 0)

    send_in(0)
    for k in range(layers):
        pltpu.make_async_copy(wc1_ref.at[k], wc1.at[k], ch_sem.at[0, k]).start()
        pltpu.make_async_copy(wc2_ref.at[k], wc2.at[k], ch_sem.at[1, k]).start()

    for copy in tok_copies:
        copy.wait()
    tile = 256

    def flip(k, carry):
        for r in range(0, patches, tile):
            w1t[k, :, r : r + tile] = s1[k, r : r + tile, :].T
        for r in range(0, tok_hidden, tile):
            w2t[k, :, r : r + tile] = s2[k, r : r + tile, :].T
        b1c[k] = jnp.broadcast_to(bt1_ref[pl.ds(k, 1), :], (128, tok_hidden)).T
        b2c[k] = jnp.broadcast_to(bt2_ref[pl.ds(k, 1), :], (128, patches)).T
        return carry

    lax.fori_loop(0, layers, flip, 0)

    def send_mid(img):
        for b in range(halves):
            def one(i, carry, b=b):
                peer = peer_at(b, turn(i))
                pltpu.make_async_remote_copy(
                    src_ref=state.at[img, pl.ds(peer * rows, rows)],
                    dst_ref=state.at[mine + img, pl.ds(b * blk + my_place * rows, rows)],
                    send_sem=mid_send.at[img],
                    recv_sem=mid_recv.at[img, b],
                    device_id={"seq": peer},
                    device_id_type=MESH,
                ).start()
                return carry

            if b == 0:
                state[mine + img, pl.ds(pl.multiple_of(my_place * rows, rows), rows), :] = state[img, pl.ds(pl.multiple_of(me * rows, rows), rows), :]
            lax.fori_loop(1 if b == 0 else 0, per_blk, one, 0)

    def arrived(slot, b, sem, count):
        at = state.at[slot, pl.ds(b * blk, count * rows)]
        pltpu.make_async_copy(at, at, sem).wait()

    def ln1_rows(slot, k, start):
        at = pl.ds(start, LN_ROWS)
        ub[at, :] = norm_rows(state[slot, at, :].astype(F32), ln_ref[k, pl.ds(0, 1), :], ln_ref[k, pl.ds(1, 1), :])

    def token_mix(slot, k):
        half = chans // 2
        for c in range(0, chans, half):
            h = jnp.dot(w1t[k], ub[:, c : c + half], preferred_element_type=F32) + b1c[k, :, 0:1]
            gb[:, c : c + half] = gelu(h).astype(BF16)
        for c in range(0, chans, half):
            t = (jnp.dot(w2t[k], gb[:, c : c + half], preferred_element_type=F32) + b2c[k, :, 0:1]).astype(BF16)
            state[slot, :, c : c + half] = (state[slot, :, c : c + half].astype(F32) + t.astype(F32)).astype(BF16)

    def ln2_rows(slot, k, b, r):
        vals = state[slot, pl.ds(b * blk + r, LN_ROWS), :].astype(F32)
        ub[pl.ds(b * blk + r, LN_ROWS), :] = norm_rows(vals, ln_ref[k, pl.ds(2, 1), :], ln_ref[k, pl.ds(3, 1), :])
        acc[pl.ds(r, LN_ROWS), :] = vals + bc2_ref[pl.ds(k, 1), :]

    def channel_mlp(slot, k, b):
        lo = pl.multiple_of(b * blk, blk)

        def up(e):
            cols = slice(e * echunk, (e + 1) * echunk)
            h = jnp.dot(ub[pl.ds(lo, blk), :], wc1[k, :, cols], preferred_element_type=F32) + bc1_ref[pl.ds(k, 1), cols]
            ab[e % 2][...] = gelu(h).astype(BF16)

        def down(e):
            return acc[...] + jnp.dot(ab[e % 2][...], wc2[k, e * echunk : (e + 1) * echunk, :], preferred_element_type=F32)

        up(0)
        for e in range(1, nchunk):
            up(e)
            acc[...] = down(e - 1)
        state[slot, pl.ds(lo, blk), :] = down(nchunk - 1).astype(BF16)

    def slot_step(slot, carry):
        k = slot // mine

        @pl.when(slot < mine)
        def _():
            for b in range(halves):
                arrived(slot, b, in_recv.at[slot, b], per_blk)

                def ln1(i, c, b=b):
                    start = pl.multiple_of(peer_at(b, i) * rows, rows)
                    for r in range(0, rows, LN_ROWS):
                        ln1_rows(slot, 0, start + r)
                    return c

                lax.fori_loop(0, per_blk, ln1, 0, unroll=UNROLL)

            @pl.when(slot + 1 < mine)
            def _():
                send_in(slot + 1)

            token_mix(slot, 0)

        @pl.when(lax.rem(slot, mine) == 0)
        def _():
            pltpu.make_async_copy(wc1_ref.at[k], wc1.at[k], ch_sem.at[0, k]).wait()
            pltpu.make_async_copy(wc2_ref.at[k], wc2.at[k], ch_sem.at[1, k]).wait()

        def block(b, c0):
            @pl.when((slot >= mine) & (b == 0))
            def _():
                arrived(slot, 0, mid_recv.at[slot - mine, 0], per_blk - 1)

            @pl.when((slot >= mine) & (b == 1))
            def _():
                arrived(slot, 1, mid_recv.at[slot - mine, 1], per_blk)

            def ln2(r, c):
                ln2_rows(slot, k, b, pl.multiple_of(r * LN_ROWS, LN_ROWS))
                return c

            lax.fori_loop(0, blk // LN_ROWS, ln2, 0, unroll=UNROLL)
            channel_mlp(slot, k, b)

            @pl.when(slot >= mine)
            def _():
                def one(place, c):
                    at = pl.ds(pl.multiple_of(b * blk + place * rows, rows), rows)
                    pltpu.make_async_copy(state.at[slot, at], out_ref.at[peer_at(b, place) * mine + slot - mine], out_sem.at[0]).start()
                    return c

                lax.fori_loop(0, per_blk, one, 0)

            return c0

        lax.fori_loop(0, halves, block, 0)

        @pl.when(slot < mine)
        def _():
            def ln1(r, c):
                ln1_rows(slot, 1, pl.multiple_of(r * LN_ROWS, LN_ROWS))
                return c

            lax.fori_loop(0, patches // LN_ROWS, ln1, 0, unroll=UNROLL)
            token_mix(slot, 1)
            send_mid(slot)

        return carry

    lax.fori_loop(0, mine * layers, slot_step, 0)

    sent = x_ref.at[pl.ds(0, n - 1)]
    for img in range(mine):
        pltpu.make_async_copy(sent, sent, in_send.at[img]).wait()
        pltpu.make_async_copy(sent, sent, mid_send.at[img]).wait()
    pltpu.make_async_copy(out_ref, out_ref, out_sem.at[0]).wait()


def solution(mesh):
    n = mesh.shape["seq"]

    def local_layers(x_blk, w_tok1, b_tok1, w_tok2, b_tok2, w_ch1, b_ch1, w_ch2, b_ch2, ln_params):
        images, rows, chans = x_blk.shape
        mine = images // n
        layers, patches, tok_hidden = w_tok1.shape
        ch_hidden = w_ch1.shape[2]
        blk = patches // 2
        hbm = pl.BlockSpec(memory_space=pl.ANY)
        vmem = pl.BlockSpec(memory_space=pltpu.VMEM)
        flops = 4 * mine * layers * patches * chans * (tok_hidden + ch_hidden)
        dma = pltpu.SemaphoreType.DMA
        return pl.pallas_call(
            functools.partial(mixer_kernel, n),
            out_shape=jax.ShapeDtypeStruct(x_blk.shape, x_blk.dtype),
            in_specs=[hbm, hbm, vmem, hbm, vmem, hbm, vmem, hbm, vmem, vmem],
            out_specs=hbm,
            scratch_shapes=[
                pltpu.VMEM((layers * mine, patches, chans), BF16),
                pltpu.VMEM((layers, tok_hidden, patches), BF16),
                pltpu.VMEM((layers, patches, tok_hidden), BF16),
                pltpu.VMEM((layers, patches, tok_hidden), BF16),
                pltpu.VMEM((layers, tok_hidden, patches), BF16),
                pltpu.VMEM((layers, chans, ch_hidden), BF16),
                pltpu.VMEM((layers, ch_hidden, chans), BF16),
                pltpu.VMEM((patches, chans), BF16),
                pltpu.VMEM((tok_hidden, chans), BF16),
                pltpu.VMEM((blk, chans), F32),
                [pltpu.VMEM((blk, ECHUNK), BF16)] * 2,
                pltpu.VMEM((layers, tok_hidden, 128), F32),
                pltpu.VMEM((layers, patches, 128), F32),
                dma((mine,)),
                dma((mine, 2)),
                dma((mine,)),
                dma((mine, 2)),
                dma((1,)),
                dma((2,)),
                dma((2, layers)),
            ],
            compiler_params=pltpu.CompilerParams(collective_id=0, has_side_effects=True, vmem_limit_bytes=67043328),
            cost_estimate=pl.CostEstimate(flops=flops, bytes_accessed=2 * x_blk.size * 2, transcendentals=0),
        )(x_blk, w_tok1, b_tok1, w_tok2, b_tok2, w_ch1, b_ch1, w_ch2, b_ch2, ln_params)

    act_spec = P("data", "seq", None)
    rep_spec = P()
    return jax.shard_map(local_layers, mesh=mesh, in_specs=(act_spec,) + (rep_spec,) * 9, out_specs=act_spec, check_vma=False)
```

time: 189 us -> 161 us (0.85)
  the two profiles are of different devices: /device:TPU:121 before, /device:TPU:97 now
where the time goes in v3:
time: 161 us
  Pallas kernels  156 us (97%)
  local copies, waits for them, and re-layouts  5.01 us (3%)
    pallas_call x1, Pallas kernels, local_layers(): pl.pallas_call(functools.partial(mixer_kernel, n), out_shape=jax.ShapeDty...  156 us
    unnamed x1, local copies, waits for them, and re-layouts  5.01 us

profile of v3, /device:TPU:97, one launch (start us, length us, event | category | flops | bytes accessed | tf_op | source)
XLA Modules:
  0.0 160.8 jit_solution(2064938875462317210)
XLA Ops:
  0.0 155.8 %shard_map.100 = bf16[64,32,1024]{2,1,0:T(8,128)(2,1)} custom-call(bf16[64,32,1024]{2,1,0:T(8,128)(2,1)} %x_ref.1, bf16[2,1024,512]{2,1,0:T(8,128)(2,1)} %wt1_ref.1, f32[2,512]{1,0:T(2,128)} %bt1_ref.1, bf16[2,512,1024]{2,1,0:T(8,128)(2,1)} %wt2_ref.1, f32[2,1024]{1,0:T(2,128)} %bt2_ref.1, bf16[2,1024,4096]{2,1,0:T(8,128)(2,1)} %wc1_ref.1, ...), custom_call_target="tpu_custom_call" | custom-call | flops 77309411328 | bytes 8388608 | tf_op jit(solution)/shard_map/pallas_call | solution.py:256
  155.8 5.0 %copy.12 = bf16[64,32,1024]{2,1,0:T(8,128)(2,1)} copy(bf16[64,32,1024]{2,1,0:T(8,128)(2,1)} %shard_map.100) | data formatting | bytes 8388608

commit v4 on v3

--- a/solution.py
+++ b/solution.py
@@ -14,7 +14,7 @@
 BF16 = jnp.bfloat16
 F32 = jnp.float32
 LN_ROWS = 16
-UNROLL = 4
+UNROLL = 16
 ECHUNK = 1024
 
 
@@ -32,7 +32,7 @@
 
 def mixer_kernel(
     n, x_ref, wt1_ref, bt1_ref, wt2_ref, bt2_ref, wc1_ref, bc1_ref, wc2_ref, bc2_ref, ln_ref,
-    out_ref, state, w1t, w2t, s1, s2, wc1, wc2, ub, gb, acc, ab, b1c, b2c,
+    out_ref, state, w1t, w2t, s1, s2, wc1, wc2, ub, vb, gb, acc, ab, b1c, b2c,
     in_send, in_recv, mid_send, mid_recv, out_sem, tok_sem, ch_sem,
 ):
     me = lax.axis_index("seq")
@@ -128,9 +128,17 @@
         at = state.at[slot, pl.ds(b * blk, count * rows)]
         pltpu.make_async_copy(at, at, sem).wait()
 
-    def ln1_rows(slot, k, start):
-        at = pl.ds(start, LN_ROWS)
-        ub[at, :] = norm_rows(state[slot, at, :].astype(F32), ln_ref[k, pl.ds(0, 1), :], ln_ref[k, pl.ds(1, 1), :])
+    def norm_at(dst, to, slot, start, k, which):
+        vals = state[slot, pl.ds(start, LN_ROWS), :].astype(F32)
+        dst[pl.ds(to, LN_ROWS), :] = norm_rows(vals, ln_ref[k, pl.ds(which, 1), :], ln_ref[k, pl.ds(which + 1, 1), :])
+
+    def norm_block(dst, to, slot, start, k, which, count):
+        def some(r, c):
+            off = pl.multiple_of(r * LN_ROWS, LN_ROWS)
+            norm_at(dst, to + off, slot, start + off, k, which)
+            return c
+
+        lax.fori_loop(0, count // LN_ROWS, some, 0, unroll=UNROLL)
 
     def token_mix(slot, k):
         half = chans // 2
@@ -141,25 +149,31 @@
             t = (jnp.dot(w2t[k], gb[:, c : c + half], preferred_element_type=F32) + b2c[k, :, 0:1]).astype(BF16)
             state[slot, :, c : c + half] = (state[slot, :, c : c + half].astype(F32) + t.astype(F32)).astype(BF16)
 
-    def ln2_rows(slot, k, b, r):
-        vals = state[slot, pl.ds(b * blk + r, LN_ROWS), :].astype(F32)
-        ub[pl.ds(b * blk + r, LN_ROWS), :] = norm_rows(vals, ln_ref[k, pl.ds(2, 1), :], ln_ref[k, pl.ds(3, 1), :])
-        acc[pl.ds(r, LN_ROWS), :] = vals + bc2_ref[pl.ds(k, 1), :]
-
     def channel_mlp(slot, k, b):
         lo = pl.multiple_of(b * blk, blk)
+        other = jnp.where((slot == mine * layers - 1) | (b == 1), 0, 1) * blk
+        side_k = jnp.minimum(k + b, layers - 1)
+        side_which = 2 * (1 - b)
+        side_rows = blk // nchunk
+
+        def side(e):
+            for r in range(e * side_rows, (e + 1) * side_rows, LN_ROWS):
+                norm_at(ub, r, slot, pl.multiple_of(other, blk) + r, side_k, side_which)
 
         def up(e):
             cols = slice(e * echunk, (e + 1) * echunk)
-            h = jnp.dot(ub[pl.ds(lo, blk), :], wc1[k, :, cols], preferred_element_type=F32) + bc1_ref[pl.ds(k, 1), cols]
+            h = jnp.dot(vb[...], wc1[k, :, cols], preferred_element_type=F32) + bc1_ref[pl.ds(k, 1), cols]
             ab[e % 2][...] = gelu(h).astype(BF16)
 
         def down(e):
-            return acc[...] + jnp.dot(ab[e % 2][...], wc2[k, e * echunk : (e + 1) * echunk, :], preferred_element_type=F32)
+            base = state[slot, pl.ds(lo, blk), :].astype(F32) + bc2_ref[pl.ds(k, 1), :] if e == 0 else acc[...]
+            return base + jnp.dot(ab[e % 2][...], wc2[k, e * echunk : (e + 1) * echunk, :], preferred_element_type=F32)
 
         up(0)
+        side(0)
         for e in range(1, nchunk):
             up(e)
+            side(e)
             acc[...] = down(e - 1)
         state[slot, pl.ds(lo, blk), :] = down(nchunk - 1).astype(BF16)
 
@@ -174,10 +188,10 @@
                 def ln1(i, c, b=b):
                     start = pl.multiple_of(peer_at(b, i) * rows, rows)
                     for r in range(0, rows, LN_ROWS):
-                        ln1_rows(slot, 0, start + r)
+                        norm_at(ub, start + r, slot, start + r, 0, 0)
                     return c
 
-                lax.fori_loop(0, per_blk, ln1, 0, unroll=UNROLL)
+                lax.fori_loop(0, per_blk, ln1, 0, unroll=min(UNROLL, per_blk))
 
             @pl.when(slot + 1 < mine)
             def _():
@@ -190,20 +204,27 @@
             pltpu.make_async_copy(wc1_ref.at[k], wc1.at[k], ch_sem.at[0, k]).wait()
             pltpu.make_async_copy(wc2_ref.at[k], wc2.at[k], ch_sem.at[1, k]).wait()
 
+        last = mine * layers - 1
+
         def block(b, c0):
+            fresh = (b == 0) | (slot == last)
+
             @pl.when((slot >= mine) & (b == 0))
             def _():
                 arrived(slot, 0, mid_recv.at[slot - mine, 0], per_blk - 1)
 
-            @pl.when((slot >= mine) & (b == 1))
+            @pl.when((slot >= mine) & ((b == 1) == (slot == last)))
             def _():
                 arrived(slot, 1, mid_recv.at[slot - mine, 1], per_blk)
 
-            def ln2(r, c):
-                ln2_rows(slot, k, b, pl.multiple_of(r * LN_ROWS, LN_ROWS))
-                return c
-
-            lax.fori_loop(0, blk // LN_ROWS, ln2, 0, unroll=UNROLL)
+            @pl.when(fresh)
+            def _():
+                norm_block(vb, 0, slot, pl.multiple_of(b * blk, blk), k, 2, blk)
+
+            @pl.when(jnp.logical_not(fresh))
+            def _():
+                vb[...] = ub[0:blk, :]
+
             channel_mlp(slot, k, b)
 
             @pl.when(slot >= mine)
@@ -221,11 +242,7 @@
 
         @pl.when(slot < mine)
         def _():
-            def ln1(r, c):
-                ln1_rows(slot, 1, pl.multiple_of(r * LN_ROWS, LN_ROWS))
-                return c
-
-            lax.fori_loop(0, patches // LN_ROWS, ln1, 0, unroll=UNROLL)
+            norm_block(ub, blk, slot, blk, 1, 0, blk)
             token_mix(slot, 1)
             send_mid(slot)
 
@@ -267,6 +284,7 @@
                 pltpu.VMEM((layers, chans, ch_hidden), BF16),
                 pltpu.VMEM((layers, ch_hidden, chans), BF16),
                 pltpu.VMEM((patches, chans), BF16),
+                pltpu.VMEM((blk, chans), BF16),
                 pltpu.VMEM((tok_hidden, chans), BF16),
                 pltpu.VMEM((blk, chans), F32),
                 [pltpu.VMEM((blk, ECHUNK), BF16)] * 2,

time: 161 us -> 149 us (0.925)
  Pallas kernels: 156 us -> 143 us
    pallas_call x1, Pallas kernels: 156 us -> 143 us  [local_layers(): pl.pallas_call(functools.partial(mixer_kernel, n), out_shape=jax.ShapeDty...]
where the time goes in v4:
time: 149 us; the launch traced here: 148 us
  Pallas kernels  143 us (96%)
  local copies, waits for them, and re-layouts  5.01 us (3%)
    pallas_call x1, Pallas kernels, local_layers(): pl.pallas_call(functools.partial(mixer_kernel, n), out_shape=jax.ShapeDty...  143 us
    unnamed x1, local copies, waits for them, and re-layouts  5.01 us

profile of v4, /device:TPU:97, one launch (start us, length us, event | category | flops | bytes accessed | tf_op | source)
XLA Modules:
  0.0 148.3 jit_solution(18077758658285960033)
XLA Ops:
  0.0 143.3 %shard_map.100 = bf16[64,32,1024]{2,1,0:T(8,128)(2,1)} custom-call(bf16[64,32,1024]{2,1,0:T(8,128)(2,1)} %x_ref.1, bf16[2,1024,512]{2,1,0:T(8,128)(2,1)} %wt1_ref.1, f32[2,512]{1,0:T(2,128)} %bt1_ref.1, bf16[2,512,1024]{2,1,0:T(8,128)(2,1)} %wt2_ref.1, f32[2,1024]{1,0:T(2,128)} %bt2_ref.1, bf16[2,1024,4096]{2,1,0:T(8,128)(2,1)} %wc1_ref.1, ...), custom_call_target="tpu_custom_call" | custom-call | flops 77309411328 | bytes 8388608 | tf_op jit(solution)/shard_map/pallas_call | solution.py:273
  143.3 5.0 %copy.12 = bf16[64,32,1024]{2,1,0:T(8,128)(2,1)} copy(bf16[64,32,1024]{2,1,0:T(8,128)(2,1)} %shard_map.100) | data formatting | bytes 8388608

commit v5 on v4

--- a/solution.py
+++ b/solution.py
@@ -15,6 +15,7 @@
 F32 = jnp.float32
 LN_ROWS = 16
 UNROLL = 16
+SENDS = 8
 ECHUNK = 1024
 
 
@@ -31,9 +32,9 @@
 
 
 def mixer_kernel(
-    n, x_ref, wt1_ref, bt1_ref, wt2_ref, bt2_ref, wc1_ref, bc1_ref, wc2_ref, bc2_ref, ln_ref,
-    out_ref, state, w1t, w2t, s1, s2, wc1, wc2, ub, vb, gb, acc, ab, b1c, b2c,
-    in_send, in_recv, mid_send, mid_recv, out_sem, tok_sem, ch_sem,
+    n, x_ref, wt1_ref, bt1_hbm, wt2_ref, bt2_hbm, wc1_ref, bc1_hbm, wc2_ref, bc2_hbm, ln_hbm,
+    out_ref, state, bt1_ref, bt2_ref, bc1_ref, bc2_ref, ln_ref, w1t, w2t, s1, s2, wc1, wc2, ub, vb, gb, acc, ab, b1c, b2c,
+    in_send, in_recv, mid_send, mid_recv, tok_sem, ch_sem, small_sem,
 ):
     me = lax.axis_index("seq")
     images, rows, chans = x_ref.shape
@@ -55,16 +56,25 @@
     def turn(i):
         return lax.rem(my_place + i * 5, per_blk)
 
+    def stage(k):
+        return pltpu.make_async_copy(wt1_ref.at[k], s1, tok_sem.at[0]), pltpu.make_async_copy(wt2_ref.at[k], s2, tok_sem.at[1])
+
+    smalls = [
+        pltpu.make_async_copy(src, dst, small_sem.at[i])
+        for i, (src, dst) in enumerate(
+            ((bt1_hbm, bt1_ref), (bt2_hbm, bt2_ref), (bc1_hbm, bc1_ref), (bc2_hbm, bc2_ref), (ln_hbm, ln_ref))
+        )
+    ]
+
     barrier = pltpu.get_barrier_semaphore()
 
     def signal_peer(i, carry):
         pl.semaphore_signal(barrier, inc=1, device_id={"seq": lax.rem(me + i, n)}, device_id_type=MESH)
         return carry
 
-    lax.fori_loop(1, n, signal_peer, 0)
-
-    tok_copies = [pltpu.make_async_copy(wt1_ref, s1, tok_sem.at[0]), pltpu.make_async_copy(wt2_ref, s2, tok_sem.at[1])]
-    for copy in tok_copies:
+    lax.fori_loop(1, n, signal_peer, 0, unroll=SENDS)
+
+    for copy in (*stage(0), *smalls):
         copy.start()
     pl.semaphore_wait(barrier, n - 1)
 
@@ -84,22 +94,30 @@
 
             if b == 0:
                 pltpu.make_async_copy(x_ref.at[me * mine + img], state.at[img, pl.ds(me * rows, rows)], in_recv.at[img, b]).start()
-            lax.fori_loop(1 if b == 0 else 0, per_blk, one, 0)
+            lax.fori_loop(1 if b == 0 else 0, per_blk, one, 0, unroll=SENDS)
 
     send_in(0)
     for k in range(layers):
         pltpu.make_async_copy(wc1_ref.at[k], wc1.at[k], ch_sem.at[0, k]).start()
         pltpu.make_async_copy(wc2_ref.at[k], wc2.at[k], ch_sem.at[1, k]).start()
 
-    for copy in tok_copies:
+    for copy in smalls:
         copy.wait()
     tile = 256
 
     def flip(k, carry):
+        for copy in stage(k):
+            copy.wait()
         for r in range(0, patches, tile):
-            w1t[k, :, r : r + tile] = s1[k, r : r + tile, :].T
+            w1t[k, :, r : r + tile] = s1[r : r + tile, :].T
         for r in range(0, tok_hidden, tile):
-            w2t[k, :, r : r + tile] = s2[k, r : r + tile, :].T
+            w2t[k, :, r : r + tile] = s2[r : r + tile, :].T
+
+        @pl.when(k + 1 < layers)
+        def _():
+            for copy in stage(k + 1):
+                copy.start()
+
         b1c[k] = jnp.broadcast_to(bt1_ref[pl.ds(k, 1), :], (128, tok_hidden)).T
         b2c[k] = jnp.broadcast_to(bt2_ref[pl.ds(k, 1), :], (128, patches)).T
         return carry
@@ -122,7 +140,7 @@
 
             if b == 0:
                 state[mine + img, pl.ds(pl.multiple_of(my_place * rows, rows), rows), :] = state[img, pl.ds(pl.multiple_of(me * rows, rows), rows), :]
-            lax.fori_loop(1 if b == 0 else 0, per_blk, one, 0)
+            lax.fori_loop(1 if b == 0 else 0, per_blk, one, 0, unroll=SENDS)
 
     def arrived(slot, b, sem, count):
         at = state.at[slot, pl.ds(b * blk, count * rows)]
@@ -231,10 +249,10 @@
             def _():
                 def one(place, c):
                     at = pl.ds(pl.multiple_of(b * blk + place * rows, rows), rows)
-                    pltpu.make_async_copy(state.at[slot, at], out_ref.at[peer_at(b, place) * mine + slot - mine], out_sem.at[0]).start()
+                    out_ref[peer_at(b, place) * mine + slot - mine] = state[slot, at, :]
                     return c
 
-                lax.fori_loop(0, per_blk, one, 0)
+                lax.fori_loop(0, per_blk, one, 0, unroll=4)
 
             return c0
 
@@ -254,7 +272,6 @@
     for img in range(mine):
         pltpu.make_async_copy(sent, sent, in_send.at[img]).wait()
         pltpu.make_async_copy(sent, sent, mid_send.at[img]).wait()
-    pltpu.make_async_copy(out_ref, out_ref, out_sem.at[0]).wait()
 
 
 def solution(mesh):
@@ -272,15 +289,20 @@
         dma = pltpu.SemaphoreType.DMA
         return pl.pallas_call(
             functools.partial(mixer_kernel, n),
-            out_shape=jax.ShapeDtypeStruct(x_blk.shape, x_blk.dtype),
-            in_specs=[hbm, hbm, vmem, hbm, vmem, hbm, vmem, hbm, vmem, vmem],
-            out_specs=hbm,
+            out_shape=pltpu.VMEM(x_blk.shape, x_blk.dtype),
+            in_specs=[hbm] * 10,
+            out_specs=vmem,
             scratch_shapes=[
                 pltpu.VMEM((layers * mine, patches, chans), BF16),
+                pltpu.VMEM(b_tok1.shape, F32),
+                pltpu.VMEM(b_tok2.shape, F32),
+                pltpu.VMEM(b_ch1.shape, F32),
+                pltpu.VMEM(b_ch2.shape, F32),
+                pltpu.VMEM(ln_params.shape, F32),
                 pltpu.VMEM((layers, tok_hidden, patches), BF16),
                 pltpu.VMEM((layers, patches, tok_hidden), BF16),
-                pltpu.VMEM((layers, patches, tok_hidden), BF16),
-                pltpu.VMEM((layers, tok_hidden, patches), BF16),
+                pltpu.VMEM((patches, tok_hidden), BF16),
+                pltpu.VMEM((tok_hidden, patches), BF16),
                 pltpu.VMEM((layers, chans, ch_hidden), BF16),
                 pltpu.VMEM((layers, ch_hidden, chans), BF16),
                 pltpu.VMEM((patches, chans), BF16),
@@ -294,11 +316,11 @@
                 dma((mine, 2)),
                 dma((mine,)),
                 dma((mine, 2)),
-                dma((1,)),
                 dma((2,)),
                 dma((2, layers)),
+                dma((5,)),
             ],
-            compiler_params=pltpu.CompilerParams(collective_id=0, has_side_effects=True, vmem_limit_bytes=67043328),
+            compiler_params=pltpu.CompilerParams(collective_id=0, has_side_effects=True, vmem_limit_bytes=62783488),
             cost_estimate=pl.CostEstimate(flops=flops, bytes_accessed=2 * x_blk.size * 2, transcendentals=0),
         )(x_blk, w_tok1, b_tok1, w_tok2, b_tok2, w_ch1, b_ch1, w_ch2, b_ch2, ln_params)
 

time: 149 us -> 145 us (0.973)
  local copies, waits for them, and re-layouts: 5.01 us -> 2.02 us
    unnamed x1, local copies, waits for them, and re-layouts: 5.01 us -> 2.02 us
where the time goes in v5:
time: 145 us
  Pallas kernels  143 us (99%)
  local copies, waits for them, and re-layouts  2.02 us (1%)
    pallas_call x1, Pallas kernels, local_layers(): pl.pallas_call(functools.partial(mixer_kernel, n), out_shape=pltpu.VMEM(x...  143 us

profile of v5, /device:TPU:97, one launch (start us, length us, event | category | flops | bytes accessed | tf_op | source)
XLA Modules:
  0.0 145.3 jit_solution(527758618292334319)
XLA Ops:
  0.0 143.2 %shard_map.100 = bf16[64,32,1024]{2,1,0:T(8,128)(2,1)S(1)} custom-call(bf16[64,32,1024]{2,1,0:T(8,128)(2,1)} %x_ref.1, bf16[2,1024,512]{2,1,0:T(8,128)(2,1)} %wt1_ref.1, f32[2,512]{1,0:T(2,128)} %bt1_hbm.1, bf16[2,512,1024]{2,1,0:T(8,128)(2,1)} %wt2_ref.1, f32[2,1024]{1,0:T(2,128)} %bt2_hbm.1, bf16[2,1024,4096]{2,1,0:T(8,128)(2,1)} %wc1_ref.1, ...), custom_call_target="tpu_custom_call" | custom-call | flops 77309411328 | bytes 8388608 | tf_op jit(solution)/shard_map/pallas_call | solution.py:290
  143.3 2.0 %copy.12 = bf16[64,32,1024]{2,1,0:T(8,128)(2,1)} copy(bf16[64,32,1024]{2,1,0:T(8,128)(2,1)S(1)} %shard_map.100) | data formatting | bytes 8388608
